TPU v7x, 32 devices: a whole 2x2x4 slice. The times are simulated.
32 devices in a mesh: blk: 8 (over y, x, core), col: 4 (over z).
Axes of the slice: x: 2, y: 2, z: 4, core: 2. Of those that a mesh axis runs over, the one named last changes fastest.
Arguments:
- samples: bfloat16 [2048, 768], P('blk'), may hold values from -3 to 3
- targets: float32 [2048, 256], P('blk'), may hold values from -6 to 6
- batch_index: int32 [1024], P('blk'), may hold values from 0 to 255
- centers: bfloat16 [4096, 768], P(('blk', 'col')), may hold values from -3 to 3
- weights: float32 [4096, 256], P(('blk', 'col')), may hold values from -6 to 6
- nystrom_index: int32 [1536], replicated, may hold values from 0 to 4095, as said below
- eigvecs: float32 [1536, 128], replicated, may hold values from -0.15625 to 0.15625
- coefficient: float32 [128], replicated, may hold values from 0.4 to 0.95
Outputs:
- residual: float32 [1024, 256], P(('blk', 'col'))
- new_weights: float32 [4096, 256], P(('blk', 'col'))
Inputs may be any that keep to these rules, and one draw needn't show every extreme that they name: Batch row i is sample row (i // 128) * 256 + batch_index[i]. `nystrom_index`: 1536 distinct center rows.
All inputs are finite; a program needn't handle non-finite values.
Results may differ from a plain program's by a relative error of at most 0.0003.
The roundings to bfloat16 on the way count: a program that leaves them out, or rounds other values in their place, can miss the bound.
Values may be sent and summed in bfloat16 or wider, within the bound.
No kernel may reach another device: no remote copies, remote signals or barrier semaphores. Data moves between devices by JAX's collectives and lax.ppermute only.
A program may use at most 64 MiB of HBM per device.

v0:
```python
import jax
import jax.numpy as jnp
from jax import lax
from jax.sharding import PartitionSpec as P

spread = 1.0
shift_sq = 1.0
step_size = 4.0


def shifted(block, axis, distance):
    devices = range(lax.axis_size(axis))
    route = [((i - distance) % len(devices), i) for i in devices]
    return lax.ppermute(block, axis, route)


def kernel_block(points, centers, center_sq):
    point_sq = jnp.sum(jnp.square(points.astype(jnp.float32)), axis=1, keepdims=True)
    cross = lax.dot_general(
        points, centers, (((1,), (1,)), ((), ())), preferred_element_type=jnp.float32
    )
    dist_sq = point_sq + center_sq[None, :] - 2.0 * cross
    return jnp.exp(-jnp.sqrt(dist_sq + shift_sq) / spread).astype(jnp.bfloat16)


def move_up(points_now):
    return shifted(points_now, "blk", 1)


def pass_up(partial_value):
    return shifted(partial_value, "blk", 1)


def local(samples, targets, batch_index, centers, weights, nystrom_index, eigvecs, coefficient):
    blocks = lax.axis_size("blk")
    columns = lax.axis_size("col")
    my_block = lax.axis_index("blk")
    blk_rows = batch_index.shape[0]
    n_center = centers.shape[0]
    out_width = weights.shape[1]
    points = jnp.take(samples, batch_index, axis=0)
    wanted = jnp.take(targets, batch_index, axis=0)
    center_sq = jnp.sum(jnp.square(centers.astype(jnp.float32)), axis=1)
    weights_low = weights.astype(jnp.bfloat16)
    kernel_store = jnp.zeros((blocks * blk_rows, n_center), jnp.bfloat16)

    def absorb(points_now, partial_value, stored, offset):
        kernel = kernel_block(points_now, centers, center_sq)
        stored = lax.dynamic_update_slice(stored, kernel, (offset, 0))
        return (
            partial_value + jnp.dot(kernel, weights_low, preferred_element_type=jnp.float32),
            stored,
        )

    def walk_step(step_idx, state_now):
        points_now, partial_value, stored = state_now
        partial_value, stored = absorb(
            points_now, partial_value, stored, (my_block - step_idx) % blocks * blk_rows
        )
        return (move_up(points_now), pass_up(partial_value), stored)

    initial = (points, jnp.zeros((blk_rows, out_width), jnp.float32), kernel_store)
    points_now, partial_value, kernel_store = lax.fori_loop(0, blocks - 1, walk_step, initial)
    partial_value, kernel_store = absorb(
        points_now, partial_value, kernel_store, (my_block + 1) % blocks * blk_rows
    )
    partial_value = pass_up(partial_value)
    share_rows = blk_rows // columns
    prediction = lax.psum(partial_value, "col")
    residual_full = prediction - wanted
    gathered = lax.all_gather(residual_full.astype(jnp.bfloat16), "blk", axis=0, tiled=True)
    own_resid = lax.dynamic_slice_in_dim(
        residual_full, lax.axis_index("col") * share_rows, share_rows, 0
    )
    gradient = lax.dot_general(
        kernel_store, gathered, (((0,), (0,)), ((), ())), preferred_element_type=jnp.float32
    )
    first_row = lax.axis_index(("blk", "col")) * n_center
    position = nystrom_index - first_row
    inside = (position >= 0) & (position < n_center)
    position = jnp.where(inside, position, n_center)
    target_row = jnp.minimum(position, n_center - 1)
    picked = jnp.where(inside[:, None], jnp.take(gradient, target_row, axis=0), 0.0)
    highest = lax.Precision.HIGHEST
    local_proj = lax.dot_general(eigvecs, picked, (((0,), (0,)), ((), ())), precision=highest)
    projected = lax.psum(local_proj, ("blk", "col"))
    correction = jnp.dot(eigvecs, coefficient[:, None] * projected, precision=highest)
    adjusted = gradient.at[position].add(-correction, mode="drop")
    return (own_resid, weights - step_size * adjusted)


def solution(mesh):
    in_specs = (
        P("blk", None),
        P("blk", None),
        P("blk"),
        P(("blk", "col"), None),
        P(("blk", "col"), None),
        P(),
        P(),
        P(),
    )
    out_specs = (P(("blk", "col"), None), P(("blk", "col"), None))
    return jax.shard_map(local, mesh=mesh, in_specs=in_specs, out_specs=out_specs, check_vma=False)
```

profile of v0, /device:TPU:0, one launch (start us, length us, event | category | flops | bytes accessed | tf_op | source)
XLA Modules:
  0.0 271.0 jit_solution(4618817647422644272)
XLA Ops:
  7.2 0.8 compare_and_fusion.2
  8.0 0.7 compare_select_fusion.2
  8.7 1.0 multiply_reduce_fusion.2
  9.7 0.9 convert_element_type.36
  10.6 2.0 gather_fusion
  12.8 53.1 %while.19 = (s32[]{:T(128)}, bf16[128,768]{1,0:T(8,128)(2,1)S(1)}, f32[128,256]{1,0:T(8,128)S(1)}, bf16[1024,128]{1,0:T(8,128)(2,1)S(1)}, f32[128]{0:T(128)S(1)}...) while((s32[]{:T(128)}, bf16[128,768]{1,0:T(8,128)(2,1)S(1)}, ...), condition=%wide.region_3.4_spmd, body=%wide.region_1.3_spmd.sunk | while | flops 33980304 | bytes 2721664 | solution.py:63
  12.9 0.5 collective-permute-start
  14.0 2.6 collective-permute-start.1
  16.6 4.4 %collective-permute-done.1 = f32[128,256]{1,0:T(8,128)S(1)} collective-permute-done((f32[128,256]{1,0:T(8,128)S(1)}, f32[128,256]{1,0:T(8,128)S(1)}, u32[]{:S(2)}, u32[]{:S(2)}) %collective-permute-start.1) | collective-permute-done | bytes 131104 | tf_op jit(solution)/shard_map/while/body/eval_jaxpr/ppermute | solution.py:14
  21.7 1.5 collective-permute-start.1
  23.2 5.3 %collective-permute-done.1 = f32[128,256]{1,0:T(8,128)S(1)} collective-permute-done((f32[128,256]{1,0:T(8,128)S(1)}, f32[128,256]{1,0:T(8,128)S(1)}, u32[]{:S(2)}, u32[]{:S(2)}) %collective-permute-start.1) | collective-permute-done | bytes 131104 | tf_op jit(solution)/shard_map/while/body/eval_jaxpr/ppermute | solution.py:14
  29.2 0.6 collective-permute-start.1
  29.7 6.2 %collective-permute-done.1 = f32[128,256]{1,0:T(8,128)S(1)} collective-permute-done((f32[128,256]{1,0:T(8,128)S(1)}, f32[128,256]{1,0:T(8,128)S(1)}, u32[]{:S(2)}, u32[]{:S(2)}) %collective-permute-start.1) | collective-permute-done | bytes 131104 | tf_op jit(solution)/shard_map/while/body/eval_jaxpr/ppermute | solution.py:14
  36.7 6.8 %collective-permute-done.1 = f32[128,256]{1,0:T(8,128)S(1)} collective-permute-done((f32[128,256]{1,0:T(8,128)S(1)}, f32[128,256]{1,0:T(8,128)S(1)}, u32[]{:S(2)}, u32[]{:S(2)}) %collective-permute-start.1) | collective-permute-done | bytes 131104 | tf_op jit(solution)/shard_map/while/body/eval_jaxpr/ppermute | solution.py:14
  44.2 6.8 %collective-permute-done.1 = f32[128,256]{1,0:T(8,128)S(1)} collective-permute-done((f32[128,256]{1,0:T(8,128)S(1)}, f32[128,256]{1,0:T(8,128)S(1)}, u32[]{:S(2)}, u32[]{:S(2)}) %collective-permute-start.1) | collective-permute-done | bytes 131104 | tf_op jit(solution)/shard_map/while/body/eval_jaxpr/ppermute | solution.py:14
  51.7 6.8 %collective-permute-done.1 = f32[128,256]{1,0:T(8,128)S(1)} collective-permute-done((f32[128,256]{1,0:T(8,128)S(1)}, f32[128,256]{1,0:T(8,128)S(1)}, u32[]{:S(2)}, u32[]{:S(2)}) %collective-permute-start.1) | collective-permute-done | bytes 131104 | tf_op jit(solution)/shard_map/while/body/eval_jaxpr/ppermute | solution.py:14
  59.1 6.8 %collective-permute-done.1 = f32[128,256]{1,0:T(8,128)S(1)} collective-permute-done((f32[128,256]{1,0:T(8,128)S(1)}, f32[128,256]{1,0:T(8,128)S(1)}, u32[]{:S(2)}, u32[]{:S(2)}) %collective-permute-start.1) | collective-permute-done | bytes 131104 | tf_op jit(solution)/shard_map/while/body/eval_jaxpr/ppermute | solution.py:14
  66.5 5.2 %collective-permute-done.2 = f32[128,256]{1,0:T(8,128)S(1)} collective-permute-done((f32[128,256]{1,0:T(8,128)S(1)}, f32[128,256]{1,0:T(8,128)S(1)}, u32[]{:S(2)}, u32[]{:S(2)}) %collective-permute-start.2) | collective-permute-done | bytes 131104 | tf_op jit(solution)/shard_map/ppermute | solution.py:14
  71.8 0.7 copy-done.4
  72.5 0.8 gather_fusion.1
  73.3 35.0 %all-reduce.3.cloned.1.call-done = f32[128,256]{1,0:T(8,128)} async-done(((f32[128,256]{1,0:T(8,128)}), f32[128,256]{1,0:T(8,128)}) %all-reduce.3.cloned.1.call-update) | async-done | bytes 131088 | tf_op jit(solution)/shard_map/psum | solution.py:69
  108.3 1.0 fusion.27
  109.3 9.8 %all_gather.3 = bf16[1024,256]{1,0:T(8,128)(2,1)S(1)} all-gather(bf16[128,256]{1,0:T(8,128)(2,1)S(1)} %get-tuple-element.224), channel_id=1, replica_groups=mesh['blk'=8,'col'=4] {'blk'}, dimensions={0}, use_global_device_ids=true | all-gather | bytes 589824 | tf_op jit(solution)/shard_map/all_gather | solution.py:71
  119.1 0.3 fusion.28
  119.4 3.7 %gather_fusion.2 = f32[1536,256]{1,0:T(8,128)S(1)} fusion(f32[128,256]{1,0:T(8,128)S(1)} %fusion.28, s32[2048]{0:T(1024)S(1)} %pad_clamp_fusion), kind=kCustom, calls=%fused_computation.2 | custom fusion | bytes 3151872 | tf_op jit(solution)/shard_map/jit(_take)/gather | solution.py:83
  123.1 2.6 fusion.10
  125.7 0.6 constant_dynamic-slice_fusion
  126.3 122.8 %all-reduce.5.cloned.1.call-done = f32[128,256]{1,0:T(8,128)} async-done(((f32[128,256]{1,0:T(8,128)}), f32[128,256]{1,0:T(8,128)}) %all-reduce.5.cloned.1.call-update) | async-done | bytes 131088 | tf_op jit(solution)/shard_map/psum | solution.py:86
  249.1 3.6 %fusion.6 = f32[1536,256]{0,1:T(8,128)} fusion(f32[1536,128]{1,0:T(8,128)S(1)} %copy-done, f32[128,256]{1,0:T(8,128)} %all-reduce.5.cloned.1.call-done, f32[128]{0:T(128)S(1)} %copy-done.6), kind=kOutput, calls=%fused_computation.15 | convolution fusion | flops 604405760 | bytes 2490880 | tf_op jit(solution)/shard_map/dot_general | solution.py:87
  252.7 1.9 copy.10
  254.6 8.9 %scatter_fusion = f32[128,256]{1,0:T(8,128)S(1)} fusion(f32[128,256]{1,0:T(8,128)S(1)} %fusion.28, s32[1536]{0:T(1024)S(1)} %compare_select_fusion.1, f32[1536,256]{1,0:T(8,128)S(1)} %copy.10), kind=kCustom, calls=%fused_computation.3 | custom fusion | flops 393216 | bytes 4724736 | tf_op jit(solution)/shard_map/scatter-add | solution.py:88
  263.5 0.7 multiply_subtract_fusion
  (73 shorter events, 5.3 us)
Async XLA Ops:
  7.2 115.9 %copy-start = (f32[1536,128]{1,0:T(8,128)S(1)}, f32[1536,128]{1,0:T(8,128)}, u32[]{:S(2)}) copy-start(f32[1536,128]{1,0:T(8,128)} %param.16) | copy-start | bytes 2359300
  7.2 5.6 %copy-start.3 = (bf16[128,768]{1,0:T(8,128)(2,1)S(1)}, bf16[128,768]{1,0:T(8,128)(2,1)}, u32[]{:S(2)}) copy-start(bf16[128,768]{1,0:T(8,128)(2,1)} %param.13) | copy-start | bytes 589828
  7.2 101.1 %all-reduce.3.cloned.1.call-start = ((), (), s32[]{:S(2)}) async-start(), calls=%async_computation | async-start | bytes 262144 | tf_op jit(solution)/shard_map/psum | solution.py:69
  12.8 53.7 %copy-start.5 = (s32[1536]{0:T(1024)S(1)}, s32[1536]{0:T(1024)}, u32[]{:S(2)}) copy-start(s32[1536]{0:T(1024)} %param.15) | copy-start | bytes 18436
  12.9 8.2 %collective-permute-start = (bf16[128,768]{1,0:T(8,128)(2,1)S(1)}, bf16[128,768]{1,0:T(8,128)(2,1)S(1)}, u32[]{:S(2)}, u32[]{:S(2)}) collective-permute-start(bf16[128,768]{1,0:T(8,128)(2,1)S(1)} %copy.17), channel_id=1, source_target_pairs={{28,0},{0,4},{4,8},{8,12},{12,16},{16,20},{20,24},{24,28},{29,1},{... | collective-permute-start | bytes 589832 | tf_op jit(solution)/shard_map/while/body/eval_jaxpr/ppermute | solution.py:14
  14.0 7.1 %collective-permute-start.1 = (f32[128,256]{1,0:T(8,128)S(1)}, f32[128,256]{1,0:T(8,128)S(1)}, u32[]{:S(2)}, u32[]{:S(2)}) collective-permute-start(f32[128,256]{1,0:T(8,128)S(1)} %convolution_add_fusion.3), channel_id=1, source_target_pairs={{28,0},{0,4},{4,8},{8,12},{12,16},{16,20},{20,24},{24,28},{29,1},{... | collective-permute-start | bytes 393224 | tf_op jit(solution)/shard_map/while/body/eval_jaxpr/ppermute | solution.py:14
  21.1 7.5 %collective-permute-start = (bf16[128,768]{1,0:T(8,128)(2,1)S(1)}, bf16[128,768]{1,0:T(8,128)(2,1)S(1)}, u32[]{:S(2)}, u32[]{:S(2)}) collective-permute-start(bf16[128,768]{1,0:T(8,128)(2,1)S(1)} %copy.17), channel_id=1, source_target_pairs={{28,0},{0,4},{4,8},{8,12},{12,16},{16,20},{20,24},{24,28},{29,1},{... | collective-permute-start | bytes 589832 | tf_op jit(solution)/shard_map/while/body/eval_jaxpr/ppermute | solution.py:14
  21.7 6.8 %collective-permute-start.1 = (f32[128,256]{1,0:T(8,128)S(1)}, f32[128,256]{1,0:T(8,128)S(1)}, u32[]{:S(2)}, u32[]{:S(2)}) collective-permute-start(f32[128,256]{1,0:T(8,128)S(1)} %convolution_add_fusion.3), channel_id=1, source_target_pairs={{28,0},{0,4},{4,8},{8,12},{12,16},{16,20},{20,24},{24,28},{29,1},{... | collective-permute-start | bytes 393224 | tf_op jit(solution)/shard_map/while/body/eval_jaxpr/ppermute | solution.py:14
  28.5 7.5 %collective-permute-start = (bf16[128,768]{1,0:T(8,128)(2,1)S(1)}, bf16[128,768]{1,0:T(8,128)(2,1)S(1)}, u32[]{:S(2)}, u32[]{:S(2)}) collective-permute-start(bf16[128,768]{1,0:T(8,128)(2,1)S(1)} %copy.17), channel_id=1, source_target_pairs={{28,0},{0,4},{4,8},{8,12},{12,16},{16,20},{20,24},{24,28},{29,1},{... | collective-permute-start | bytes 589832 | tf_op jit(solution)/shard_map/while/body/eval_jaxpr/ppermute | solution.py:14
  29.2 6.8 %collective-permute-start.1 = (f32[128,256]{1,0:T(8,128)S(1)}, f32[128,256]{1,0:T(8,128)S(1)}, u32[]{:S(2)}, u32[]{:S(2)}) collective-permute-start(f32[128,256]{1,0:T(8,128)S(1)} %convolution_add_fusion.3), channel_id=1, source_target_pairs={{28,0},{0,4},{4,8},{8,12},{12,16},{16,20},{20,24},{24,28},{29,1},{... | collective-permute-start | bytes 393224 | tf_op jit(solution)/shard_map/while/body/eval_jaxpr/ppermute | solution.py:14
  36.0 7.5 %collective-permute-start = (bf16[128,768]{1,0:T(8,128)(2,1)S(1)}, bf16[128,768]{1,0:T(8,128)(2,1)S(1)}, u32[]{:S(2)}, u32[]{:S(2)}) collective-permute-start(bf16[128,768]{1,0:T(8,128)(2,1)S(1)} %copy.17), channel_id=1, source_target_pairs={{28,0},{0,4},{4,8},{8,12},{12,16},{16,20},{20,24},{24,28},{29,1},{... | collective-permute-start | bytes 589832 | tf_op jit(solution)/shard_map/while/body/eval_jaxpr/ppermute | solution.py:14
  36.6 6.8 %collective-permute-start.1 = (f32[128,256]{1,0:T(8,128)S(1)}, f32[128,256]{1,0:T(8,128)S(1)}, u32[]{:S(2)}, u32[]{:S(2)}) collective-permute-start(f32[128,256]{1,0:T(8,128)S(1)} %convolution_add_fusion.3), channel_id=1, source_target_pairs={{28,0},{0,4},{4,8},{8,12},{12,16},{16,20},{20,24},{24,28},{29,1},{... | collective-permute-start | bytes 393224 | tf_op jit(solution)/shard_map/while/body/eval_jaxpr/ppermute | solution.py:14
  43.5 7.5 %collective-permute-start = (bf16[128,768]{1,0:T(8,128)(2,1)S(1)}, bf16[128,768]{1,0:T(8,128)(2,1)S(1)}, u32[]{:S(2)}, u32[]{:S(2)}) collective-permute-start(bf16[128,768]{1,0:T(8,128)(2,1)S(1)} %copy.17), channel_id=1, source_target_pairs={{28,0},{0,4},{4,8},{8,12},{12,16},{16,20},{20,24},{24,28},{29,1},{... | collective-permute-start | bytes 589832 | tf_op jit(solution)/shard_map/while/body/eval_jaxpr/ppermute | solution.py:14
  44.1 6.8 %collective-permute-start.1 = (f32[128,256]{1,0:T(8,128)S(1)}, f32[128,256]{1,0:T(8,128)S(1)}, u32[]{:S(2)}, u32[]{:S(2)}) collective-permute-start(f32[128,256]{1,0:T(8,128)S(1)} %convolution_add_fusion.3), channel_id=1, source_target_pairs={{28,0},{0,4},{4,8},{8,12},{12,16},{16,20},{20,24},{24,28},{29,1},{... | collective-permute-start | bytes 393224 | tf_op jit(solution)/shard_map/while/body/eval_jaxpr/ppermute | solution.py:14
  51.0 7.5 %collective-permute-start = (bf16[128,768]{1,0:T(8,128)(2,1)S(1)}, bf16[128,768]{1,0:T(8,128)(2,1)S(1)}, u32[]{:S(2)}, u32[]{:S(2)}) collective-permute-start(bf16[128,768]{1,0:T(8,128)(2,1)S(1)} %copy.17), channel_id=1, source_target_pairs={{28,0},{0,4},{4,8},{8,12},{12,16},{16,20},{20,24},{24,28},{29,1},{... | collective-permute-start | bytes 589832 | tf_op jit(solution)/shard_map/while/body/eval_jaxpr/ppermute | solution.py:14
  51.6 6.8 %collective-permute-start.1 = (f32[128,256]{1,0:T(8,128)S(1)}, f32[128,256]{1,0:T(8,128)S(1)}, u32[]{:S(2)}, u32[]{:S(2)}) collective-permute-start(f32[128,256]{1,0:T(8,128)S(1)} %convolution_add_fusion.3), channel_id=1, source_target_pairs={{28,0},{0,4},{4,8},{8,12},{12,16},{16,20},{20,24},{24,28},{29,1},{... | collective-permute-start | bytes 393224 | tf_op jit(solution)/shard_map/while/body/eval_jaxpr/ppermute | solution.py:14
  58.4 7.5 %collective-permute-start = (bf16[128,768]{1,0:T(8,128)(2,1)S(1)}, bf16[128,768]{1,0:T(8,128)(2,1)S(1)}, u32[]{:S(2)}, u32[]{:S(2)}) collective-permute-start(bf16[128,768]{1,0:T(8,128)(2,1)S(1)} %copy.17), channel_id=1, source_target_pairs={{28,0},{0,4},{4,8},{8,12},{12,16},{16,20},{20,24},{24,28},{29,1},{... | collective-permute-start | bytes 589832 | tf_op jit(solution)/shard_map/while/body/eval_jaxpr/ppermute | solution.py:14
  59.1 6.8 %collective-permute-start.1 = (f32[128,256]{1,0:T(8,128)S(1)}, f32[128,256]{1,0:T(8,128)S(1)}, u32[]{:S(2)}, u32[]{:S(2)}) collective-permute-start(f32[128,256]{1,0:T(8,128)S(1)} %convolution_add_fusion.3), channel_id=1, source_target_pairs={{28,0},{0,4},{4,8},{8,12},{12,16},{16,20},{20,24},{24,28},{29,1},{... | collective-permute-start | bytes 393224 | tf_op jit(solution)/shard_map/while/body/eval_jaxpr/ppermute | solution.py:14
  65.9 6.6 %copy-start.1 = (f32[256,256]{1,0:T(8,128)S(1)}, f32[256,256]{1,0:T(8,128)}, u32[]{:S(2)}) copy-start(f32[256,256]{1,0:T(8,128)} %param.11) | copy-start | bytes 786436
  66.4 5.3 %collective-permute-start.2 = (f32[128,256]{1,0:T(8,128)S(1)}, f32[128,256]{1,0:T(8,128)S(1)}, u32[]{:S(2)}, u32[]{:S(2)}) collective-permute-start(f32[128,256]{1,0:T(8,128)S(1)} %convolution_add_fusion.1), channel_id=1, source_target_pairs={{28,0},{0,4},{4,8},{8,12},{12,16},{16,20},{20,24},{24,28},{29,1},{... | collective-permute-start | bytes 393224 | tf_op jit(solution)/shard_map/ppermute | solution.py:14
  71.8 0.7 copy-start.4
  72.4 176.6 %all-reduce.5.cloned.1.call-start = ((), (), s32[]{:S(2)}) async-start(), calls=%async_computation.1 | async-start | bytes 262144 | tf_op jit(solution)/shard_map/psum | solution.py:86
  123.1 126.0 %copy-start.6 = (f32[128]{0:T(128)S(1)}, f32[128]{0:T(128)}, u32[]{:S(2)}) copy-start(f32[128]{0:T(128)} %param.17) | copy-start | bytes 1540
  254.6 8.9 %copy-start.2 = (f32[128,256]{1,0:T(8,128)S(1)}, f32[128,256]{1,0:T(8,128)}, u32[]{:S(2)}) copy-start(f32[128,256]{1,0:T(8,128)} %param.14) | copy-start | bytes 393220
Sparse Core Ops, SparseCore 0:
  72.6 35.7 all-reduce.2
  125.8 123.2 all-reduce.4
where the time goes:
time: 271 us
  waiting for transfers between devices  206 us (76%)
  other arithmetic  15 us (6%)
  between operations  14.3 us (5%)
  blocking collectives  9.79 us (4%)
  local copies, waits for them, and re-layouts  9.77 us (4%)
  matrix products  9.7 us (4%)
  starting transfers between devices  5.97 us (2%)
    psum x1, waiting for transfers between devices, local(): projected = lax.psum(local_proj, ('blk', 'col'))  123 us
    ppermute x15, waiting for transfers between devices, shifted(): return lax.ppermute(block, axis, route)  48.3 us
    psum x1, waiting for transfers between devices, local(): prediction = lax.psum(partial_value, 'col')  35 us
    all_gather x1, blocking collectives, local(): lax.all_gather(residual_full.astype(jnp.bfloat16), 'blk', axis=0, tiled=T...  9.79 us
    scatter-add x1, other arithmetic, local(): adjusted = gradient.at[position].add(-correction, mode='drop')  8.88 us
    ppermute x15, starting transfers between devices, shifted(): return lax.ppermute(block, axis, route)  5.89 us
  transfers between devices with their start and end apart: 17, of which 10 were waited for; matrix products, arithmetic and copies ran while one was open for 2% of the time, Pallas kernels for 0%

commit v1 on v0

--- a/solution.py
+++ b/solution.py
@@ -83,7 +83,7 @@
     picked = jnp.where(inside[:, None], jnp.take(gradient, target_row, axis=0), 0.0)
     highest = lax.Precision.HIGHEST
     local_proj = lax.dot_general(eigvecs, picked, (((0,), (0,)), ((), ())), precision=highest)
-    projected = lax.psum(local_proj, ("blk", "col"))
+    projected = lax.psum(lax.psum(local_proj, "col"), "blk")
     correction = jnp.dot(eigvecs, coefficient[:, None] * projected, precision=highest)
     adjusted = gradient.at[position].add(-correction, mode="drop")
     return (own_resid, weights - step_size * adjusted)

time: 271 us -> 237 us (0.87)
  waiting for transfers between devices: 206 us -> 172 us
    psum x1 -> x2, waiting for transfers between devices: 123 us -> 89.1 us  [local(): projected = lax.psum(lax.psum(local_proj, 'col'), 'blk')]
  transfers between devices with their start and end apart: 17 -> 18, of which waited for: 10 -> 11; matrix products, arithmetic and copies ran while one was open for 2% -> 2% of each run, Pallas kernels for 0% -> 0%
where the time goes in v1:
time: 237 us
  waiting for transfers between devices  172 us (73%)
  other arithmetic  15 us (6%)
  between operations  14 us (6%)
  blocking collectives  9.79 us (4%)
  local copies, waits for them, and re-layouts  9.77 us (4%)
  matrix products  9.69 us (4%)
  starting transfers between devices  6.01 us (3%)
    psum x2, waiting for transfers between devices, local(): projected = lax.psum(lax.psum(local_proj, 'col'), 'blk')  89.1 us
    ppermute x15, waiting for transfers between devices, shifted(): return lax.ppermute(block, axis, route)  48.4 us
    psum x1, waiting for transfers between devices, local(): prediction = lax.psum(partial_value, 'col')  35 us
    all_gather x1, blocking collectives, local(): lax.all_gather(residual_full.astype(jnp.bfloat16), 'blk', axis=0, tiled=T...  9.79 us
    scatter-add x1, other arithmetic, local(): adjusted = gradient.at[position].add(-correction, mode='drop')  8.88 us
    ppermute x15, starting transfers between devices, shifted(): return lax.ppermute(block, axis, route)  5.88 us
  transfers between devices with their start and end apart: 18, of which 11 were waited for; matrix products, arithmetic and copies ran while one was open for 2% of the time, Pallas kernels for 0%

profile of v1, /device:TPU:0, one launch (start us, length us, event | category | flops | bytes accessed | tf_op | source)
XLA Modules:
  0.0 237.0 jit_solution(137709659229433875)
XLA Ops:
  7.2 0.8 compare_and_fusion.2
  8.0 0.7 compare_select_fusion.2
  8.7 1.0 multiply_reduce_fusion.2
  9.7 0.9 convert_element_type.36
  10.6 2.0 gather_fusion
  12.8 53.1 %while.19 = (s32[]{:T(128)}, bf16[128,768]{1,0:T(8,128)(2,1)S(1)}, f32[128,256]{1,0:T(8,128)S(1)}, bf16[1024,128]{1,0:T(8,128)(2,1)S(1)}, f32[128]{0:T(128)S(1)}...) while((s32[]{:T(128)}, bf16[128,768]{1,0:T(8,128)(2,1)S(1)}, ...), condition=%wide.region_3.4_spmd, body=%wide.region_1.3_spmd.sunk | while | flops 33980304 | bytes 2721664 | solution.py:63
  12.9 0.5 collective-permute-start
  14.0 2.6 %collective-permute-start.1 = (f32[128,256]{1,0:T(8,128)S(1)}, f32[128,256]{1,0:T(8,128)S(1)}, u32[]{:S(2)}, u32[]{:S(2)}) collective-permute-start(f32[128,256]{1,0:T(8,128)S(1)} %convolution_add_fusion.3), channel_id=1, source_target_pairs={{28,0},{0,4},{4,8},{8,12},{12,16},{16,20},{20,24},{24,28},{29,1},{... | collective-permute-start | bytes 393224 | tf_op jit(solution)/shard_map/while/body/eval_jaxpr/ppermute | solution.py:14
  16.6 4.4 %collective-permute-done.1 = f32[128,256]{1,0:T(8,128)S(1)} collective-permute-done((f32[128,256]{1,0:T(8,128)S(1)}, f32[128,256]{1,0:T(8,128)S(1)}, u32[]{:S(2)}, u32[]{:S(2)}) %collective-permute-start.1) | collective-permute-done | bytes 131104 | tf_op jit(solution)/shard_map/while/body/eval_jaxpr/ppermute | solution.py:14
  21.7 1.5 collective-permute-start.1
  23.2 5.3 %collective-permute-done.1 = f32[128,256]{1,0:T(8,128)S(1)} collective-permute-done((f32[128,256]{1,0:T(8,128)S(1)}, f32[128,256]{1,0:T(8,128)S(1)}, u32[]{:S(2)}, u32[]{:S(2)}) %collective-permute-start.1) | collective-permute-done | bytes 131104 | tf_op jit(solution)/shard_map/while/body/eval_jaxpr/ppermute | solution.py:14
  29.2 0.6 collective-permute-start.1
  29.7 6.2 %collective-permute-done.1 = f32[128,256]{1,0:T(8,128)S(1)} collective-permute-done((f32[128,256]{1,0:T(8,128)S(1)}, f32[128,256]{1,0:T(8,128)S(1)}, u32[]{:S(2)}, u32[]{:S(2)}) %collective-permute-start.1) | collective-permute-done | bytes 131104 | tf_op jit(solution)/shard_map/while/body/eval_jaxpr/ppermute | solution.py:14
  36.7 6.8 %collective-permute-done.1 = f32[128,256]{1,0:T(8,128)S(1)} collective-permute-done((f32[128,256]{1,0:T(8,128)S(1)}, f32[128,256]{1,0:T(8,128)S(1)}, u32[]{:S(2)}, u32[]{:S(2)}) %collective-permute-start.1) | collective-permute-done | bytes 131104 | tf_op jit(solution)/shard_map/while/body/eval_jaxpr/ppermute | solution.py:14
  44.2 6.8 %collective-permute-done.1 = f32[128,256]{1,0:T(8,128)S(1)} collective-permute-done((f32[128,256]{1,0:T(8,128)S(1)}, f32[128,256]{1,0:T(8,128)S(1)}, u32[]{:S(2)}, u32[]{:S(2)}) %collective-permute-start.1) | collective-permute-done | bytes 131104 | tf_op jit(solution)/shard_map/while/body/eval_jaxpr/ppermute | solution.py:14
  51.7 6.8 %collective-permute-done.1 = f32[128,256]{1,0:T(8,128)S(1)} collective-permute-done((f32[128,256]{1,0:T(8,128)S(1)}, f32[128,256]{1,0:T(8,128)S(1)}, u32[]{:S(2)}, u32[]{:S(2)}) %collective-permute-start.1) | collective-permute-done | bytes 131104 | tf_op jit(solution)/shard_map/while/body/eval_jaxpr/ppermute | solution.py:14
  59.1 6.8 %collective-permute-done.1 = f32[128,256]{1,0:T(8,128)S(1)} collective-permute-done((f32[128,256]{1,0:T(8,128)S(1)}, f32[128,256]{1,0:T(8,128)S(1)}, u32[]{:S(2)}, u32[]{:S(2)}) %collective-permute-start.1) | collective-permute-done | bytes 131104 | tf_op jit(solution)/shard_map/while/body/eval_jaxpr/ppermute | solution.py:14
  66.5 5.3 %collective-permute-done.2 = f32[128,256]{1,0:T(8,128)S(1)} collective-permute-done((f32[128,256]{1,0:T(8,128)S(1)}, f32[128,256]{1,0:T(8,128)S(1)}, u32[]{:S(2)}, u32[]{:S(2)}) %collective-permute-start.2) | collective-permute-done | bytes 131104 | tf_op jit(solution)/shard_map/ppermute | solution.py:14
  71.8 0.7 copy-done.4
  72.5 0.8 gather_fusion.1
  73.3 35.0 %all-reduce.4.cloned.1.call-done = f32[128,256]{1,0:T(8,128)} async-done(((f32[128,256]{1,0:T(8,128)}), f32[128,256]{1,0:T(8,128)}) %all-reduce.4.cloned.1.call-update) | async-done | bytes 131088 | tf_op jit(solution)/shard_map/psum | solution.py:69
  108.3 1.0 fusion.27
  109.3 9.8 %all_gather.3 = bf16[1024,256]{1,0:T(8,128)(2,1)S(1)} all-gather(bf16[128,256]{1,0:T(8,128)(2,1)S(1)} %get-tuple-element.224), channel_id=1, replica_groups=mesh['blk'=8,'col'=4] {'blk'}, dimensions={0}, use_global_device_ids=true | all-gather | bytes 589824 | tf_op jit(solution)/shard_map/all_gather | solution.py:71
  119.4 3.7 %gather_fusion.2 = f32[1536,256]{1,0:T(8,128)S(1)} fusion(f32[128,256]{1,0:T(8,128)S(1)} %fusion.28, s32[2048]{0:T(1024)S(1)} %pad_clamp_fusion), kind=kCustom, calls=%fused_computation.2 | custom fusion | bytes 3151872 | tf_op jit(solution)/shard_map/jit(_take)/gather | solution.py:83
  123.1 2.6 %fusion.10 = f32[128,256]{1,0:T(8,128)} fusion(f32[1536,128]{1,0:T(8,128)S(1)} %copy-done, f32[1536,256]{1,0:T(8,128)S(1)} %gather_fusion.2, pred[1536]{0:T(1024)(128)(4,1)S(1)} %get-tuple-element.222, pred[1536]{0:T(1024)(128)(4,1)S(1)} %get-tuple-element.228), kind=kOutput, calls=%fused_computation.19 | convolution fusion | flops 604766208 | bytes 2493440 | tf_op jit(solution)/shard_map/dot_general | solution.py:85
  125.7 33.5 %all-reduce.6.cloned.1.call-done = f32[128,256]{1,0:T(8,128)} async-done(((f32[128,256]{1,0:T(8,128)}), f32[128,256]{1,0:T(8,128)}) %all-reduce.6.cloned.1.call-update) | async-done | bytes 131088 | tf_op jit(solution)/shard_map/psum | solution.py:86
  159.3 0.6 constant_dynamic-slice_fusion
  159.9 55.5 %all-reduce.8.cloned.1.call-done = f32[128,256]{1,0:T(8,128)} async-done(((f32[128,256]{1,0:T(8,128)}), f32[128,256]{1,0:T(8,128)}) %all-reduce.8.cloned.1.call-update) | async-done | bytes 131088 | tf_op jit(solution)/shard_map/psum | solution.py:86
  215.5 3.6 %fusion.6 = f32[1536,256]{0,1:T(8,128)} fusion(f32[1536,128]{1,0:T(8,128)S(1)} %copy-done, f32[128,256]{1,0:T(8,128)} %all-reduce.8.cloned.1.call-done, f32[128]{0:T(128)S(1)} %copy-done.6), kind=kOutput, calls=%fused_computation.15 | convolution fusion | flops 604405760 | bytes 2490880 | tf_op jit(solution)/shard_map/dot_general | solution.py:87
  219.0 1.9 copy.10
  220.9 8.9 %scatter_fusion = f32[128,256]{1,0:T(8,128)S(1)} fusion(f32[128,256]{1,0:T(8,128)S(1)} %fusion.28, s32[1536]{0:T(1024)S(1)} %compare_select_fusion.1, f32[1536,256]{1,0:T(8,128)S(1)} %copy.10), kind=kCustom, calls=%fused_computation.3 | custom fusion | flops 393216 | bytes 4724736 | tf_op jit(solution)/shard_map/scatter-add | solution.py:88
  229.8 0.7 multiply_subtract_fusion
  (76 shorter events, 5.6 us)
Async XLA Ops:
  7.2 115.9 %copy-start = (f32[1536,128]{1,0:T(8,128)S(1)}, f32[1536,128]{1,0:T(8,128)}, u32[]{:S(2)}) copy-start(f32[1536,128]{1,0:T(8,128)} %param.16) | copy-start | bytes 2359300
  7.2 5.6 %copy-start.3 = (bf16[128,768]{1,0:T(8,128)(2,1)S(1)}, bf16[128,768]{1,0:T(8,128)(2,1)}, u32[]{:S(2)}) copy-start(bf16[128,768]{1,0:T(8,128)(2,1)} %param.13) | copy-start | bytes 589828
  7.2 101.1 %all-reduce.4.cloned.1.call-start = ((), (), s32[]{:S(2)}) async-start(), calls=%async_computation | async-start | bytes 262144 | tf_op jit(solution)/shard_map/psum | solution.py:69
  12.8 59.7 %copy-start.5 = (s32[1536]{0:T(1024)S(1)}, s32[1536]{0:T(1024)}, u32[]{:S(2)}) copy-start(s32[1536]{0:T(1024)} %param.15) | copy-start | bytes 18436
  12.9 8.2 %collective-permute-start = (bf16[128,768]{1,0:T(8,128)(2,1)S(1)}, bf16[128,768]{1,0:T(8,128)(2,1)S(1)}, u32[]{:S(2)}, u32[]{:S(2)}) collective-permute-start(bf16[128,768]{1,0:T(8,128)(2,1)S(1)} %copy.17), channel_id=1, source_target_pairs={{28,0},{0,4},{4,8},{8,12},{12,16},{16,20},{20,24},{24,28},{29,1},{... | collective-permute-start | bytes 589832 | tf_op jit(solution)/shard_map/while/body/eval_jaxpr/ppermute | solution.py:14
  14.0 7.1 %collective-permute-start.1 = (f32[128,256]{1,0:T(8,128)S(1)}, f32[128,256]{1,0:T(8,128)S(1)}, u32[]{:S(2)}, u32[]{:S(2)}) collective-permute-start(f32[128,256]{1,0:T(8,128)S(1)} %convolution_add_fusion.3), channel_id=1, source_target_pairs={{28,0},{0,4},{4,8},{8,12},{12,16},{16,20},{20,24},{24,28},{29,1},{... | collective-permute-start | bytes 393224 | tf_op jit(solution)/shard_map/while/body/eval_jaxpr/ppermute | solution.py:14
  21.1 7.5 %collective-permute-start = (bf16[128,768]{1,0:T(8,128)(2,1)S(1)}, bf16[128,768]{1,0:T(8,128)(2,1)S(1)}, u32[]{:S(2)}, u32[]{:S(2)}) collective-permute-start(bf16[128,768]{1,0:T(8,128)(2,1)S(1)} %copy.17), channel_id=1, source_target_pairs={{28,0},{0,4},{4,8},{8,12},{12,16},{16,20},{20,24},{24,28},{29,1},{... | collective-permute-start | bytes 589832 | tf_op jit(solution)/shard_map/while/body/eval_jaxpr/ppermute | solution.py:14
  21.7 6.8 %collective-permute-start.1 = (f32[128,256]{1,0:T(8,128)S(1)}, f32[128,256]{1,0:T(8,128)S(1)}, u32[]{:S(2)}, u32[]{:S(2)}) collective-permute-start(f32[128,256]{1,0:T(8,128)S(1)} %convolution_add_fusion.3), channel_id=1, source_target_pairs={{28,0},{0,4},{4,8},{8,12},{12,16},{16,20},{20,24},{24,28},{29,1},{... | collective-permute-start | bytes 393224 | tf_op jit(solution)/shard_map/while/body/eval_jaxpr/ppermute | solution.py:14
  28.5 7.5 %collective-permute-start = (bf16[128,768]{1,0:T(8,128)(2,1)S(1)}, bf16[128,768]{1,0:T(8,128)(2,1)S(1)}, u32[]{:S(2)}, u32[]{:S(2)}) collective-permute-start(bf16[128,768]{1,0:T(8,128)(2,1)S(1)} %copy.17), channel_id=1, source_target_pairs={{28,0},{0,4},{4,8},{8,12},{12,16},{16,20},{20,24},{24,28},{29,1},{... | collective-permute-start | bytes 589832 | tf_op jit(solution)/shard_map/while/body/eval_jaxpr/ppermute | solution.py:14
  29.2 6.8 %collective-permute-start.1 = (f32[128,256]{1,0:T(8,128)S(1)}, f32[128,256]{1,0:T(8,128)S(1)}, u32[]{:S(2)}, u32[]{:S(2)}) collective-permute-start(f32[128,256]{1,0:T(8,128)S(1)} %convolution_add_fusion.3), channel_id=1, source_target_pairs={{28,0},{0,4},{4,8},{8,12},{12,16},{16,20},{20,24},{24,28},{29,1},{... | collective-permute-start | bytes 393224 | tf_op jit(solution)/shard_map/while/body/eval_jaxpr/ppermute | solution.py:14
  36.0 7.5 %collective-permute-start = (bf16[128,768]{1,0:T(8,128)(2,1)S(1)}, bf16[128,768]{1,0:T(8,128)(2,1)S(1)}, u32[]{:S(2)}, u32[]{:S(2)}) collective-permute-start(bf16[128,768]{1,0:T(8,128)(2,1)S(1)} %copy.17), channel_id=1, source_target_pairs={{28,0},{0,4},{4,8},{8,12},{12,16},{16,20},{20,24},{24,28},{29,1},{... | collective-permute-start | bytes 589832 | tf_op jit(solution)/shard_map/while/body/eval_jaxpr/ppermute | solution.py:14
  36.6 6.8 %collective-permute-start.1 = (f32[128,256]{1,0:T(8,128)S(1)}, f32[128,256]{1,0:T(8,128)S(1)}, u32[]{:S(2)}, u32[]{:S(2)}) collective-permute-start(f32[128,256]{1,0:T(8,128)S(1)} %convolution_add_fusion.3), channel_id=1, source_target_pairs={{28,0},{0,4},{4,8},{8,12},{12,16},{16,20},{20,24},{24,28},{29,1},{... | collective-permute-start | bytes 393224 | tf_op jit(solution)/shard_map/while/body/eval_jaxpr/ppermute | solution.py:14
  43.5 7.5 %collective-permute-start = (bf16[128,768]{1,0:T(8,128)(2,1)S(1)}, bf16[128,768]{1,0:T(8,128)(2,1)S(1)}, u32[]{:S(2)}, u32[]{:S(2)}) collective-permute-start(bf16[128,768]{1,0:T(8,128)(2,1)S(1)} %copy.17), channel_id=1, source_target_pairs={{28,0},{0,4},{4,8},{8,12},{12,16},{16,20},{20,24},{24,28},{29,1},{... | collective-permute-start | bytes 589832 | tf_op jit(solution)/shard_map/while/body/eval_jaxpr/ppermute | solution.py:14
  44.1 6.8 %collective-permute-start.1 = (f32[128,256]{1,0:T(8,128)S(1)}, f32[128,256]{1,0:T(8,128)S(1)}, u32[]{:S(2)}, u32[]{:S(2)}) collective-permute-start(f32[128,256]{1,0:T(8,128)S(1)} %convolution_add_fusion.3), channel_id=1, source_target_pairs={{28,0},{0,4},{4,8},{8,12},{12,16},{16,20},{20,24},{24,28},{29,1},{... | collective-permute-start | bytes 393224 | tf_op jit(solution)/shard_map/while/body/eval_jaxpr/ppermute | solution.py:14
  51.0 7.5 %collective-permute-start = (bf16[128,768]{1,0:T(8,128)(2,1)S(1)}, bf16[128,768]{1,0:T(8,128)(2,1)S(1)}, u32[]{:S(2)}, u32[]{:S(2)}) collective-permute-start(bf16[128,768]{1,0:T(8,128)(2,1)S(1)} %copy.17), channel_id=1, source_target_pairs={{28,0},{0,4},{4,8},{8,12},{12,16},{16,20},{20,24},{24,28},{29,1},{... | collective-permute-start | bytes 589832 | tf_op jit(solution)/shard_map/while/body/eval_jaxpr/ppermute | solution.py:14
  51.6 6.8 %collective-permute-start.1 = (f32[128,256]{1,0:T(8,128)S(1)}, f32[128,256]{1,0:T(8,128)S(1)}, u32[]{:S(2)}, u32[]{:S(2)}) collective-permute-start(f32[128,256]{1,0:T(8,128)S(1)} %convolution_add_fusion.3), channel_id=1, source_target_pairs={{28,0},{0,4},{4,8},{8,12},{12,16},{16,20},{20,24},{24,28},{29,1},{... | collective-permute-start | bytes 393224 | tf_op jit(solution)/shard_map/while/body/eval_jaxpr/ppermute | solution.py:14
  58.4 7.5 %collective-permute-start = (bf16[128,768]{1,0:T(8,128)(2,1)S(1)}, bf16[128,768]{1,0:T(8,128)(2,1)S(1)}, u32[]{:S(2)}, u32[]{:S(2)}) collective-permute-start(bf16[128,768]{1,0:T(8,128)(2,1)S(1)} %copy.17), channel_id=1, source_target_pairs={{28,0},{0,4},{4,8},{8,12},{12,16},{16,20},{20,24},{24,28},{29,1},{... | collective-permute-start | bytes 589832 | tf_op jit(solution)/shard_map/while/body/eval_jaxpr/ppermute | solution.py:14
  59.1 6.8 %collective-permute-start.1 = (f32[128,256]{1,0:T(8,128)S(1)}, f32[128,256]{1,0:T(8,128)S(1)}, u32[]{:S(2)}, u32[]{:S(2)}) collective-permute-start(f32[128,256]{1,0:T(8,128)S(1)} %convolution_add_fusion.3), channel_id=1, source_target_pairs={{28,0},{0,4},{4,8},{8,12},{12,16},{16,20},{20,24},{24,28},{29,1},{... | collective-permute-start | bytes 393224 | tf_op jit(solution)/shard_map/while/body/eval_jaxpr/ppermute | solution.py:14
  65.9 6.7 %copy-start.1 = (f32[256,256]{1,0:T(8,128)S(1)}, f32[256,256]{1,0:T(8,128)}, u32[]{:S(2)}) copy-start(f32[256,256]{1,0:T(8,128)} %param.11) | copy-start | bytes 786436
  66.4 5.3 %collective-permute-start.2 = (f32[128,256]{1,0:T(8,128)S(1)}, f32[128,256]{1,0:T(8,128)S(1)}, u32[]{:S(2)}, u32[]{:S(2)}) collective-permute-start(f32[128,256]{1,0:T(8,128)S(1)} %convolution_add_fusion.1), channel_id=1, source_target_pairs={{28,0},{0,4},{4,8},{8,12},{12,16},{16,20},{20,24},{24,28},{29,1},{... | collective-permute-start | bytes 393224 | tf_op jit(solution)/shard_map/ppermute | solution.py:14
  71.8 0.7 copy-start.4
  72.4 86.8 %all-reduce.6.cloned.1.call-start = ((), (), s32[]{:S(2)}) async-start(), calls=%async_computation.1 | async-start | bytes 262144 | tf_op jit(solution)/shard_map/psum | solution.py:86
  123.1 92.4 %copy-start.6 = (f32[128]{0:T(128)S(1)}, f32[128]{0:T(128)}, u32[]{:S(2)}) copy-start(f32[128]{0:T(128)} %param.17) | copy-start | bytes 1540
  125.7 89.8 %all-reduce.8.cloned.1.call-start = ((), (), s32[]{:S(2)}) async-start(), calls=%async_computation.2 | async-start | bytes 262144 | tf_op jit(solution)/shard_map/psum | solution.py:86
  220.9 8.9 %copy-start.2 = (f32[128,256]{1,0:T(8,128)S(1)}, f32[128,256]{1,0:T(8,128)}, u32[]{:S(2)}) copy-start(f32[128,256]{1,0:T(8,128)} %param.14) | copy-start | bytes 393220
Sparse Core Ops, SparseCore 0:
  72.6 35.7 all-reduce.3
  125.8 33.4 all-reduce.5
  162.3 53.0 all-reduce.7
